TPU v7x, 32 devices: a whole 2x2x4 slice. The times are simulated.
32 devices in a mesh: tm: 16 (over z, y, core), asset: 2 (over x).
Axes of the slice: x: 2, y: 2, z: 4, core: 2. Of those that a mesh axis runs over, the one named last changes fastest.
Arguments:
- tick_bars: float32 [2, 16, 61440], P('asset', 'tm'), may hold values from -20 to 20
- prior_bars: float32 [2, 16, 6400], P('asset', 'tm'), may hold values from -20 to 20, as said below
Outputs:
- connectedness: float32 [48, 8192], P('tm', 'asset')
Inputs may be any that keep to these rules, and one draw needn't show every extreme that they name: `prior_bars`: bar returns of the same assets.
All inputs are finite; a program needn't handle non-finite values.
Results may differ from a plain program's by a relative error of at most 0.0014.
Values may be sent and summed in bfloat16 or wider, within the bound.
A program may use at most 64 MiB of HBM per device.

v0:
```python
import math
import jax
import jax.numpy as jnp
from jax import lax
from jax.sharding import PartitionSpec as P

ASSETS = 8192
SPAN = 30
STRIDE = 5
WIN_DEV = 3
LEAD = 25
FLOOR_SQUARES = 1.0


def from_behind(x, axis, by):
    size = lax.axis_size(axis)
    pairs = [(i, i + by) for i in range(size) if 0 <= i + by < size]
    return lax.ppermute(x, axis, pairs)


def swapped(block, axis, distance):
    count = lax.axis_size(axis)
    route = []
    for low in range(count):
        high = low | 1 << distance
        if high != low and high < count:
            route += [(low, high), (high, low)]
    return lax.ppermute(block, axis, route)


def window_stack(extended):
    columns = extended.shape[1]
    groups = extended.reshape(-1, STRIDE, columns)
    stacked = jnp.stack(
        [groups[offset : offset + WIN_DEV] for offset in range(SPAN // STRIDE)], axis=1
    )
    values = stacked.reshape(WIN_DEV, SPAN, columns)
    centred = values - jnp.mean(values, axis=1, keepdims=True)
    squares = jnp.sum(centred * centred, axis=1, keepdims=True)
    return (centred * lax.rsqrt(jnp.maximum(squares, FLOOR_SQUARES))).astype(jnp.bfloat16)


def block_magnitude(left_part, right_part, offset, block_rows):
    correlation = lax.dot_general(
        left_part[:, offset : offset + block_rows],
        right_part,
        (((0,), (0,)), ((), ())),
        preferred_element_type=jnp.float32,
    )
    return jnp.abs(correlation.astype(jnp.bfloat16)).astype(jnp.float32)


def row_totals(own_windows, other_windows):
    columns = own_windows.shape[2]
    block_rows = min(1024, columns)

    def row_one_window(operands):
        left_part, right_part = operands
        pieces = [
            jnp.sum(block_magnitude(left_part, right_part, offset, block_rows), axis=1)
            for offset in range(0, columns, block_rows)
        ]
        return jnp.concatenate(pieces)

    return lax.map(row_one_window, (own_windows, other_windows))


def both_totals(own_windows, other_windows):
    columns = own_windows.shape[2]
    block_rows = min(1024, columns)

    def both_one_window(operands):
        left_part, right_part = operands
        pieces = []
        column_total = jnp.zeros((right_part.shape[1],), jnp.float32)
        for offset in range(0, columns, block_rows):
            magnitude = block_magnitude(left_part, right_part, offset, block_rows)
            pieces.append(jnp.sum(magnitude, axis=1))
            column_total = column_total + jnp.sum(magnitude, axis=0)
        return (jnp.concatenate(pieces), column_total)

    return lax.map(both_one_window, (own_windows, other_windows))


def earlier_rows(tail_rows, distance):
    return from_behind(tail_rows, "tm", distance)


def time_block_rows(tick_bars, prior_bars):
    groups = lax.axis_size("tm")
    group_cols = ASSETS // (2 * groups)
    outgoing = tick_bars.reshape(groups, 1, -1)
    arrived = lax.all_to_all(outgoing, "tm", split_axis=0, concat_axis=1, tiled=True)
    block_len = arrived.shape[2] // group_cols
    own_rows = jnp.transpose(arrived.reshape(groups, block_len, group_cols), (1, 0, 2)).reshape(
        block_len, groups * group_cols
    )
    prior_all = lax.all_gather(prior_bars, "tm", axis=1, tiled=True)
    series_prior = jnp.transpose(prior_all.reshape(groups, LEAD, group_cols), (1, 0, 2)).reshape(
        LEAD, groups * group_cols
    )
    reach = (LEAD + block_len - 1) // block_len
    earlier = []
    for distance in range(reach, 0, -1):
        needed = min(block_len, LEAD - (distance - 1) * block_len)
        earlier.append(earlier_rows(own_rows[block_len - needed :], distance))
    history = jnp.concatenate(earlier, axis=0)
    position = lax.axis_index("tm")
    first_row = position * block_len
    padded = jnp.concatenate([series_prior, jnp.zeros_like(series_prior)], axis=0)
    from_prior = lax.dynamic_slice_in_dim(padded, jnp.minimum(first_row, LEAD), LEAD, 0)
    before_start = first_row - LEAD + jnp.arange(LEAD, dtype=jnp.int32) < 0
    history = jnp.where(before_start[:, None], from_prior, history)
    return jnp.concatenate([history, own_rows], axis=0)


def shards(tick_bars, prior_bars):
    extended = time_block_rows(tick_bars, prior_bars)
    scaled = window_stack(extended)
    columns = scaled.shape[2]
    empty = jnp.zeros((WIN_DEV, columns), jnp.float32)
    partner = swapped(scaled, "asset", 0)
    tile_index = lax.axis_index("asset")
    quarter = columns // 2
    diagonal_part = row_totals(scaled, scaled)
    column_part = empty
    cross_rows = []
    for half_index in range(2):
        mine = scaled[:, :, half_index * quarter : (half_index + 1) * quarter]
        target = (half_index + tile_index) % 2
        theirs = lax.dynamic_slice_in_dim(partner, target * quarter, quarter, 2)
        row_add, column_add = both_totals(mine, theirs)
        cross_rows.append(row_add)
        column_part = lax.dynamic_update_slice_in_dim(column_part, column_add, target * quarter, 1)
    returned = swapped(column_part.astype(jnp.bfloat16), "asset", 0).astype(column_part.dtype)
    totals = diagonal_part + jnp.concatenate(cross_rows, axis=1) + returned
    return totals * (math.sqrt(SPAN) / ASSETS)


def solution(mesh):
    in_specs = (P("asset", "tm", None), P("asset", "tm", None))
    out_specs = P("tm", "asset")
    return jax.shard_map(shards, mesh=mesh, in_specs=in_specs, out_specs=out_specs, check_vma=False)
```

profile of v0, /device:TPU:0, one launch (start us, length us, event | category | flops | bytes accessed | tf_op | source)
XLA Modules:
  0.0 132.5 jit_solution(15997069284028944891)
XLA Ops:
  0.0 7.5 %all-to-all-start = ((f32[16,1,3840]{2,1,0:T(1,128)}), f32[16,1,3840]{2,1,0:T(1,128)S(1)}, u32[]{:S(2)}, u32[]{:S(2)}) async-start(f32[16,1,3840]{2,1,0:T(1,128)} %bitcast.93), calls=%async_computation | async-start | bytes 491520 | tf_op jit(solution)/shard_map/all_to_all | solution.py:93
  7.6 9.8 %all-to-all-done = f32[16,1,3840]{2,1,0:T(1,128)S(1)} async-done(((f32[16,1,3840]{2,1,0:T(1,128)}), f32[16,1,3840]{2,1,0:T(1,128)S(1)}, u32[]{:S(2)}, u32[]{:S(2)}) %all-to-all-start) | async-done | bytes 245792 | tf_op jit(solution)/shard_map/all_to_all | solution.py:93
  17.3 0.6 reduce.9
  18.0 0.1 copy.12
  18.2 0.2 copy.17
  18.3 1.8 %collective-permute-start.1 = (f32[15,4096]{1,0:T(8,128)S(1)}, f32[15,4096]{1,0:T(8,128)S(1)}, u32[]{:S(2)}, u32[]{:S(2)}) collective-permute-start(f32[15,4096]{1,0:T(8,128)S(1)} %bitcast.86), channel_id=1, source_target_pairs={{0,2},{2,4},{4,6},{6,8},{8,10},{10,12},{12,14},{14,16},{16,18},{18... | collective-permute-start | bytes 737288 | tf_op jit(solution)/shard_map/ppermute | solution.py:18
  20.3 0.2 copy.16
  20.4 2.5 %collective-permute-start = (f32[10,4096]{1,0:T(8,128)S(1)}, f32[10,4096]{1,0:T(8,128)S(1)}, u32[]{:S(2)}, u32[]{:S(2)}) collective-permute-start(f32[10,4096]{1,0:T(8,128)S(1)} %bitcast.92), channel_id=1, source_target_pairs={{0,4},{2,6},{4,8},{6,10},{8,12},{10,14},{12,16},{14,18},{16,20},{1... | collective-permute-start | bytes 491528 | tf_op jit(solution)/shard_map/ppermute | solution.py:18
  23.0 22.3 %all_gather.3 = f32[1,16,6400]{2,0,1:T(1,128)S(1)} all-gather(f32[1,1,6400]{2,0,1:T(1,128)S(1)} %bitcast.94), channel_id=1, replica_groups=mesh['tm'=16,'asset'=2] {'tm'}, dimensions={1}, use_global_device_ids=true | all-gather | bytes 435200 | tf_op jit(solution)/shard_map/all_gather | solution.py:98
  45.3 1.0 reduce.8
  46.3 0.2 copy.10
  46.6 0.3 copy.15
  47.1 0.1 fusion.20
  47.2 1.1 pad_maximum_fusion.3
  48.3 0.8 fusion.25
  49.1 1.7 %stack.22 = f32[3,1,5,4096]{3,2,0,1:T(8,128)} reshape(f32[15,4096]{1,0:T(8,128)} %get-tuple-element.124) | data formatting | bytes 491520 | tf_op jit(solution)/shard_map/stack | solution.py:34
  50.8 1.7 %stack.23 = f32[3,1,5,4096]{3,2,0,1:T(8,128)} reshape(f32[15,4096]{1,0:T(8,128)} %get-tuple-element.123) | data formatting | bytes 491520 | tf_op jit(solution)/shard_map/stack | solution.py:34
  52.6 1.0 stack.24
  53.5 1.0 stack.25
  54.5 1.1 fusion.24
  55.7 1.1 fusion.26
  56.8 0.1 fusion.27
  57.0 0.1 fusion.28
  57.1 0.1 fusion.29
  57.3 1.6 %copy.14 = f32[3,6,5,4096]{3,2,1,0:T(8,128)} copy(f32[3,6,5,4096]{3,2,0,1:T(8,128)S(1)} %get-tuple-element.137) | data formatting | bytes 2949120 | tf_op jit(solution)/shard_map/stack | solution.py:34
  59.0 0.4 multiply_reduce_fusion
  59.4 1.7 %reshape.86 = f32[3,30,4096]{2,1,0:T(8,128)S(1)} reshape(f32[3,6,5,4096]{3,2,1,0:T(8,128)} %copy.14) | data formatting | bytes 2949120 | tf_op jit(solution)/shard_map/reshape | solution.py:37
  61.1 0.2 multiply_convert_fusion
  61.3 1.6 %collective-permute-start.2 = (bf16[3,30,4096]{2,1,0:T(8,128)(2,1)S(1)}, bf16[3,30,4096]{2,1,0:T(8,128)(2,1)S(1)}, u32[]{:S(2)}, u32[]{:S(2)}) collective-permute-start(bf16[3,30,4096]{2,1,0:T(8,128)(2,1)S(1)} %multiply_convert_fusion), channel_id=1, source_target_pairs={{0,1},{1,0},{2,3},{3,2},{4,5},{5,4},{6,7},{7,6},{8,9},{9,8},{10,11... | collective-permute-start | bytes 2211848 | tf_op jit(solution)/shard_map/ppermute | solution.py:28
  62.9 18.2 %collective-permute-done.2 = bf16[3,30,4096]{2,1,0:T(8,128)(2,1)S(1)} collective-permute-done((bf16[3,30,4096]{2,1,0:T(8,128)(2,1)S(1)}, bf16[3,30,4096]{2,1,0:T(8,128)(2,1)S(1)}, u32[]{:S(2)}, u32[]{:S(2)}) %collective-permute-start.2) | collective-permute-done | bytes 737312 | tf_op jit(solution)/shard_map/ppermute | solution.py:28
  81.3 9.1 %while.35 = (s32[]{:T(128)}, f32[3,2048]{1,0:T(4,128)S(1)}, f32[3,2048]{1,0:T(4,128)S(1)}, bf16[3,30,2048]{2,1,0:T(8,128)(2,1)S(1)}, bf16[3,30,2048]{2,1,0:T(8,128)(2,1)S(1)}, /*index=5*/s32[]{:T(128)}, s32[]{:T(128)}) while((s32[]{:T(128)}, f32[3,2048]{1,0:T(4,128)S(1)}, f32[3,2048]{1,0:T(4,128)S(1)}, bf16[3,30,2048]{2,1,0:T(8,128)(2,1)S(1)}, ...), condition=%wide.region_18.19_spmd, body=%wide.region_13.18_spmd.sunk | while | flops 272627712 | bytes 737377 | solution.py:82
  81.3 1.4 %convert_reduce_fusion.25 = (f32[2048]{0:T(1024)S(1)}, f32[1024]{0:T(1024)S(1)}) fusion(bf16[3,30,2048]{2,1,0:T(8,128)(2,1)S(1)} %get-tuple-element.289, s32[]{:T(128)} %get-tuple-element.278, bf16[30,2048]{1,0:T(8,128)(2,1)S(1)} %dynamic-slice_bitcast_fusion.7), kind=kOutput, calls=%fused_computation.12.clone.1 | convolution fusion | flops 136311808 | bytes 208900 | tf_op jit(solution)/shard_map/while/body/eval_jaxpr/dot_general | solution.py:44
  82.7 1.4 %convert_reduce_fusion.24 = (f32[2048]{0:T(1024)S(1)}, f32[1024]{0:T(1024)S(1)}) fusion(bf16[3,30,2048]{2,1,0:T(8,128)(2,1)S(1)} %get-tuple-element.289, s32[]{:T(128)} %get-tuple-element.278, bf16[30,2048]{1,0:T(8,128)(2,1)S(1)} %dynamic-slice_bitcast_fusion.7), kind=kOutput, calls=%fused_computation.10.clone.1 | convolution fusion | flops 136311808 | bytes 208900 | tf_op jit(solution)/shard_map/while/body/eval_jaxpr/dot_general | solution.py:44
  84.0 0.1 dynamic_update_slice.34
  84.2 0.1 dynamic_update_slice.33
  84.3 1.4 %convert_reduce_fusion.25 = (f32[2048]{0:T(1024)S(1)}, f32[1024]{0:T(1024)S(1)}) fusion(bf16[3,30,2048]{2,1,0:T(8,128)(2,1)S(1)} %get-tuple-element.289, s32[]{:T(128)} %get-tuple-element.278, bf16[30,2048]{1,0:T(8,128)(2,1)S(1)} %dynamic-slice_bitcast_fusion.7), kind=kOutput, calls=%fused_computation.12.clone.1 | convolution fusion | flops 136311808 | bytes 208900 | tf_op jit(solution)/shard_map/while/body/eval_jaxpr/dot_general | solution.py:44
  85.7 1.4 %convert_reduce_fusion.24 = (f32[2048]{0:T(1024)S(1)}, f32[1024]{0:T(1024)S(1)}) fusion(bf16[3,30,2048]{2,1,0:T(8,128)(2,1)S(1)} %get-tuple-element.289, s32[]{:T(128)} %get-tuple-element.278, bf16[30,2048]{1,0:T(8,128)(2,1)S(1)} %dynamic-slice_bitcast_fusion.7), kind=kOutput, calls=%fused_computation.10.clone.1 | convolution fusion | flops 136311808 | bytes 208900 | tf_op jit(solution)/shard_map/while/body/eval_jaxpr/dot_general | solution.py:44
  87.4 1.4 %convert_reduce_fusion.25 = (f32[2048]{0:T(1024)S(1)}, f32[1024]{0:T(1024)S(1)}) fusion(bf16[3,30,2048]{2,1,0:T(8,128)(2,1)S(1)} %get-tuple-element.289, s32[]{:T(128)} %get-tuple-element.278, bf16[30,2048]{1,0:T(8,128)(2,1)S(1)} %dynamic-slice_bitcast_fusion.7), kind=kOutput, calls=%fused_computation.12.clone.1 | convolution fusion | flops 136311808 | bytes 208900 | tf_op jit(solution)/shard_map/while/body/eval_jaxpr/dot_general | solution.py:44
  88.7 1.4 %convert_reduce_fusion.24 = (f32[2048]{0:T(1024)S(1)}, f32[1024]{0:T(1024)S(1)}) fusion(bf16[3,30,2048]{2,1,0:T(8,128)(2,1)S(1)} %get-tuple-element.289, s32[]{:T(128)} %get-tuple-element.278, bf16[30,2048]{1,0:T(8,128)(2,1)S(1)} %dynamic-slice_bitcast_fusion.7), kind=kOutput, calls=%fused_computation.10.clone.1 | convolution fusion | flops 136311808 | bytes 208900 | tf_op jit(solution)/shard_map/while/body/eval_jaxpr/dot_general | solution.py:44
  90.4 9.2 %while.36 = (s32[]{:T(128)}, f32[3,2048]{1,0:T(4,128)S(1)}, f32[3,2048]{1,0:T(4,128)S(1)}, bf16[3,30,2048]{2,1,0:T(8,128)(2,1)S(1)}, bf16[3,30,2048]{2,1,0:T(8,128)(2,1)S(1)}, /*index=5*/s32[]{:T(128)}, s32[]{:T(128)}) while((s32[]{:T(128)}, f32[3,2048]{1,0:T(4,128)S(1)}, f32[3,2048]{1,0:T(4,128)S(1)}, bf16[3,30,2048]{2,1,0:T(8,128)(2,1)S(1)}, ...), condition=%wide.region_24.25_spmd, body=%wide.region_19.24_spmd.sunk | while | flops 272627712 | bytes 737377 | solution.py:82
  90.5 1.4 %convert_reduce_fusion.27 = (f32[2048]{0:T(1024)S(1)}, f32[1024]{0:T(1024)S(1)}) fusion(bf16[3,30,2048]{2,1,0:T(8,128)(2,1)S(1)} %get-tuple-element.268, s32[]{:T(128)} %get-tuple-element.257, bf16[30,2048]{1,0:T(8,128)(2,1)S(1)} %dynamic-slice_bitcast_fusion.8), kind=kOutput, calls=%fused_computation.28.clone.1 | convolution fusion | flops 136311808 | bytes 208900 | tf_op jit(solution)/shard_map/while/body/eval_jaxpr/dot_general | solution.py:44
  91.8 1.4 %convert_reduce_fusion.26 = (f32[2048]{0:T(1024)S(1)}, f32[1024]{0:T(1024)S(1)}) fusion(bf16[3,30,2048]{2,1,0:T(8,128)(2,1)S(1)} %get-tuple-element.268, s32[]{:T(128)} %get-tuple-element.257, bf16[30,2048]{1,0:T(8,128)(2,1)S(1)} %dynamic-slice_bitcast_fusion.8), kind=kOutput, calls=%fused_computation.26.clone.1 | convolution fusion | flops 136311808 | bytes 208900 | tf_op jit(solution)/shard_map/while/body/eval_jaxpr/dot_general | solution.py:44
  93.5 1.4 %convert_reduce_fusion.27 = (f32[2048]{0:T(1024)S(1)}, f32[1024]{0:T(1024)S(1)}) fusion(bf16[3,30,2048]{2,1,0:T(8,128)(2,1)S(1)} %get-tuple-element.268, s32[]{:T(128)} %get-tuple-element.257, bf16[30,2048]{1,0:T(8,128)(2,1)S(1)} %dynamic-slice_bitcast_fusion.8), kind=kOutput, calls=%fused_computation.28.clone.1 | convolution fusion | flops 136311808 | bytes 208900 | tf_op jit(solution)/shard_map/while/body/eval_jaxpr/dot_general | solution.py:44
  94.9 1.4 %convert_reduce_fusion.26 = (f32[2048]{0:T(1024)S(1)}, f32[1024]{0:T(1024)S(1)}) fusion(bf16[3,30,2048]{2,1,0:T(8,128)(2,1)S(1)} %get-tuple-element.268, s32[]{:T(128)} %get-tuple-element.257, bf16[30,2048]{1,0:T(8,128)(2,1)S(1)} %dynamic-slice_bitcast_fusion.8), kind=kOutput, calls=%fused_computation.26.clone.1 | convolution fusion | flops 136311808 | bytes 208900 | tf_op jit(solution)/shard_map/while/body/eval_jaxpr/dot_general | solution.py:44
  96.6 1.4 %convert_reduce_fusion.27 = (f32[2048]{0:T(1024)S(1)}, f32[1024]{0:T(1024)S(1)}) fusion(bf16[3,30,2048]{2,1,0:T(8,128)(2,1)S(1)} %get-tuple-element.268, s32[]{:T(128)} %get-tuple-element.257, bf16[30,2048]{1,0:T(8,128)(2,1)S(1)} %dynamic-slice_bitcast_fusion.8), kind=kOutput, calls=%fused_computation.28.clone.1 | convolution fusion | flops 136311808 | bytes 208900 | tf_op jit(solution)/shard_map/while/body/eval_jaxpr/dot_general | solution.py:44
  97.9 1.4 %convert_reduce_fusion.26 = (f32[2048]{0:T(1024)S(1)}, f32[1024]{0:T(1024)S(1)}) fusion(bf16[3,30,2048]{2,1,0:T(8,128)(2,1)S(1)} %get-tuple-element.268, s32[]{:T(128)} %get-tuple-element.257, bf16[30,2048]{1,0:T(8,128)(2,1)S(1)} %dynamic-slice_bitcast_fusion.8), kind=kOutput, calls=%fused_computation.26.clone.1 | convolution fusion | flops 136311808 | bytes 208900 | tf_op jit(solution)/shard_map/while/body/eval_jaxpr/dot_general | solution.py:44
  99.7 1.6 %collective-permute-start.3 = (bf16[3,4096]{1,0:T(4,128)(2,1)S(1)}, bf16[3,4096]{1,0:T(4,128)(2,1)S(1)}, u32[]{:S(2)}, u32[]{:S(2)}) collective-permute-start(bf16[3,4096]{1,0:T(4,128)(2,1)S(1)} %convert_element_type.58), channel_id=1, source_target_pairs={{0,1},{1,0},{2,3},{3,2},{4,5},{5,4},{6,7},{7,6},{8,9},{9,8},{10,11... | collective-permute-start | bytes 73736 | tf_op jit(solution)/shard_map/ppermute | solution.py:28
  101.3 30.5 %while.34 = (s32[]{:T(128)}, f32[3,4096]{1,0:T(4,128)S(1)}, bf16[3,30,4096]{2,1,0:T(8,128)(2,1)S(1)}, s32[]{:T(128)}, s32[]{:T(128)}) while((s32[]{:T(128)}, f32[3,4096]{1,0:T(4,128)S(1)}, bf16[3,30,4096]{2,1,0:T(8,128)(2,1)S(1)}, s32[]{:T(128)}, s32[]{:T(128)}) %tuple.68), condition=%wide.region_12.13_spmd, body=%wide.region_7.12_spmd.sunk | while | flops 1073750016 | bytes 1884229 | solution.py:65
  101.5 2.4 %convert_reduce_fusion.20 = f32[1024]{0:T(1024)S(1)} fusion(bf16[30,4096]{1,0:T(8,128)(2,1)S(1)} %dynamic-slice_bitcast_fusion.6), kind=kOutput, calls=%fused_computation.clone.1 | convolution fusion | flops 268434432 | bytes 331776 | tf_op jit(solution)/shard_map/while/body/eval_jaxpr/dot_general | solution.py:44
  104.0 2.5 %convert_reduce_fusion.21 = f32[1024]{0:T(1024)S(1)} fusion(bf16[30,4096]{1,0:T(8,128)(2,1)S(1)} %dynamic-slice_bitcast_fusion.6), kind=kOutput, calls=%fused_computation.1.clone.1 | convolution fusion | flops 268434432 | bytes 331776 | tf_op jit(solution)/shard_map/while/body/eval_jaxpr/dot_general | solution.py:44
  106.4 2.5 %convert_reduce_fusion.22 = f32[1024]{0:T(1024)S(1)} fusion(bf16[30,4096]{1,0:T(8,128)(2,1)S(1)} %dynamic-slice_bitcast_fusion.6), kind=kOutput, calls=%fused_computation.2.clone.1 | convolution fusion | flops 268434432 | bytes 331776 | tf_op jit(solution)/shard_map/while/body/eval_jaxpr/dot_general | solution.py:44
  108.9 2.5 %convert_reduce_fusion.23 = f32[1024]{0:T(1024)S(1)} fusion(bf16[30,4096]{1,0:T(8,128)(2,1)S(1)} %dynamic-slice_bitcast_fusion.6), kind=kOutput, calls=%fused_computation.3.clone.1 | convolution fusion | flops 268434432 | bytes 331776 | tf_op jit(solution)/shard_map/while/body/eval_jaxpr/dot_general | solution.py:44
  111.3 0.2 dynamic_update_slice.32
  111.6 2.4 %convert_reduce_fusion.20 = f32[1024]{0:T(1024)S(1)} fusion(bf16[30,4096]{1,0:T(8,128)(2,1)S(1)} %dynamic-slice_bitcast_fusion.6), kind=kOutput, calls=%fused_computation.clone.1 | convolution fusion | flops 268434432 | bytes 331776 | tf_op jit(solution)/shard_map/while/body/eval_jaxpr/dot_general | solution.py:44
  114.1 2.5 %convert_reduce_fusion.21 = f32[1024]{0:T(1024)S(1)} fusion(bf16[30,4096]{1,0:T(8,128)(2,1)S(1)} %dynamic-slice_bitcast_fusion.6), kind=kOutput, calls=%fused_computation.1.clone.1 | convolution fusion | flops 268434432 | bytes 331776 | tf_op jit(solution)/shard_map/while/body/eval_jaxpr/dot_general | solution.py:44
  116.5 2.5 %convert_reduce_fusion.22 = f32[1024]{0:T(1024)S(1)} fusion(bf16[30,4096]{1,0:T(8,128)(2,1)S(1)} %dynamic-slice_bitcast_fusion.6), kind=kOutput, calls=%fused_computation.2.clone.1 | convolution fusion | flops 268434432 | bytes 331776 | tf_op jit(solution)/shard_map/while/body/eval_jaxpr/dot_general | solution.py:44
  119.0 2.5 %convert_reduce_fusion.23 = f32[1024]{0:T(1024)S(1)} fusion(bf16[30,4096]{1,0:T(8,128)(2,1)S(1)} %dynamic-slice_bitcast_fusion.6), kind=kOutput, calls=%fused_computation.3.clone.1 | convolution fusion | flops 268434432 | bytes 331776 | tf_op jit(solution)/shard_map/while/body/eval_jaxpr/dot_general | solution.py:44
  121.4 0.2 dynamic_update_slice.32
  121.7 2.4 %convert_reduce_fusion.20 = f32[1024]{0:T(1024)S(1)} fusion(bf16[30,4096]{1,0:T(8,128)(2,1)S(1)} %dynamic-slice_bitcast_fusion.6), kind=kOutput, calls=%fused_computation.clone.1 | convolution fusion | flops 268434432 | bytes 331776 | tf_op jit(solution)/shard_map/while/body/eval_jaxpr/dot_general | solution.py:44
  124.2 2.5 %convert_reduce_fusion.21 = f32[1024]{0:T(1024)S(1)} fusion(bf16[30,4096]{1,0:T(8,128)(2,1)S(1)} %dynamic-slice_bitcast_fusion.6), kind=kOutput, calls=%fused_computation.1.clone.1 | convolution fusion | flops 268434432 | bytes 331776 | tf_op jit(solution)/shard_map/while/body/eval_jaxpr/dot_general | solution.py:44
  126.6 2.5 %convert_reduce_fusion.22 = f32[1024]{0:T(1024)S(1)} fusion(bf16[30,4096]{1,0:T(8,128)(2,1)S(1)} %dynamic-slice_bitcast_fusion.6), kind=kOutput, calls=%fused_computation.2.clone.1 | convolution fusion | flops 268434432 | bytes 331776 | tf_op jit(solution)/shard_map/while/body/eval_jaxpr/dot_general | solution.py:44
  129.1 2.5 %convert_reduce_fusion.23 = f32[1024]{0:T(1024)S(1)} fusion(bf16[30,4096]{1,0:T(8,128)(2,1)S(1)} %dynamic-slice_bitcast_fusion.6), kind=kOutput, calls=%fused_computation.3.clone.1 | convolution fusion | flops 268434432 | bytes 331776 | tf_op jit(solution)/shard_map/while/body/eval_jaxpr/dot_general | solution.py:44
  131.6 0.2 dynamic_update_slice.32
  131.8 0.7 fusion.22
  (64 shorter events, 2.3 us)
Async XLA Ops:
  0.0 23.0 %copy-start.1 = (f32[1,1,6400]{2,1,0:T(1,128)S(1)}, f32[1,1,6400]{2,1,0:T(1,128)}, u32[]{:S(2)}) copy-start(f32[1,1,6400]{2,1,0:T(1,128)} %param.9) | copy-start | bytes 76804
  0.0 17.3 %all-to-all-start = ((f32[16,1,3840]{2,1,0:T(1,128)}), f32[16,1,3840]{2,1,0:T(1,128)S(1)}, u32[]{:S(2)}, u32[]{:S(2)}) async-start(f32[16,1,3840]{2,1,0:T(1,128)} %bitcast.93), calls=%async_computation | async-start | bytes 491520 | tf_op jit(solution)/shard_map/all_to_all | solution.py:93
  18.3 28.7 %collective-permute-start.1 = (f32[15,4096]{1,0:T(8,128)S(1)}, f32[15,4096]{1,0:T(8,128)S(1)}, u32[]{:S(2)}, u32[]{:S(2)}) collective-permute-start(f32[15,4096]{1,0:T(8,128)S(1)} %bitcast.86), channel_id=1, source_target_pairs={{0,2},{2,4},{4,6},{6,8},{8,10},{10,12},{12,14},{14,16},{16,18},{18... | collective-permute-start | bytes 737288 | tf_op jit(solution)/shard_map/ppermute | solution.py:18
  20.4 26.6 %collective-permute-start = (f32[10,4096]{1,0:T(8,128)S(1)}, f32[10,4096]{1,0:T(8,128)S(1)}, u32[]{:S(2)}, u32[]{:S(2)}) collective-permute-start(f32[10,4096]{1,0:T(8,128)S(1)} %bitcast.92), channel_id=1, source_target_pairs={{0,4},{2,6},{4,8},{6,10},{8,12},{10,14},{12,16},{14,18},{16,20},{1... | collective-permute-start | bytes 491528 | tf_op jit(solution)/shard_map/ppermute | solution.py:18
  57.3 1.6 %copy-start = (f32[3,4096]{1,0:T(4,128)S(1)}, f32[3,4096]{1,0:T(4,128)}, u32[]{:S(2)}) copy-start(f32[3,4096]{1,0:T(4,128)} %get-tuple-element.128) | copy-start | bytes 147460
  61.3 19.9 %collective-permute-start.2 = (bf16[3,30,4096]{2,1,0:T(8,128)(2,1)S(1)}, bf16[3,30,4096]{2,1,0:T(8,128)(2,1)S(1)}, u32[]{:S(2)}, u32[]{:S(2)}) collective-permute-start(bf16[3,30,4096]{2,1,0:T(8,128)(2,1)S(1)} %multiply_convert_fusion), channel_id=1, source_target_pairs={{0,1},{1,0},{2,3},{3,2},{4,5},{5,4},{6,7},{7,6},{8,9},{9,8},{10,11... | collective-permute-start | bytes 2211848 | tf_op jit(solution)/shard_map/ppermute | solution.py:28
  99.7 32.1 %collective-permute-start.3 = (bf16[3,4096]{1,0:T(4,128)(2,1)S(1)}, bf16[3,4096]{1,0:T(4,128)(2,1)S(1)}, u32[]{:S(2)}, u32[]{:S(2)}) collective-permute-start(bf16[3,4096]{1,0:T(4,128)(2,1)S(1)} %convert_element_type.58), channel_id=1, source_target_pairs={{0,1},{1,0},{2,3},{3,2},{4,5},{5,4},{6,7},{7,6},{8,9},{9,8},{10,11... | collective-permute-start | bytes 73736 | tf_op jit(solution)/shard_map/ppermute | solution.py:28
where the time goes:
time: 133 us; the launch traced here: 132 us
  matrix products  45.7 us (34%)
  waiting for transfers between devices  28 us (21%)
  blocking collectives  22.3 us (17%)
  starting transfers between devices  15 us (11%)
  local copies, waits for them, and re-layouts  12.9 us (10%)
  other arithmetic  7.66 us (6%)
    dot_general x24, matrix products, block_magnitude(): lax.dot_general(left_part[:, offset:offset + block_rows], right_part, (((...  45.7 us
    all_gather x1, blocking collectives, time_block_rows(): prior_all = lax.all_gather(prior_bars, 'tm', axis=1, tiled=True)  22.3 us
    ppermute x2, waiting for transfers between devices, swapped(): return lax.ppermute(block, axis, route)  18.2 us
    all_to_all x1, waiting for transfers between devices, time_block_rows(): lax.all_to_all(outgoing, 'tm', split_axis=0, concat_axis=1, tiled=True)  9.75 us
    all_to_all x1, starting transfers between devices, time_block_rows(): lax.all_to_all(outgoing, 'tm', split_axis=0, concat_axis=1, tiled=True)  7.55 us
    another operation x7, local copies, waits for them, and re-layouts, window_stack(): jnp.stack([groups[offset:offset + WIN_DEV] for offset in range(SPAN // ST...  7.1 us
    ppermute x2, starting transfers between devices, from_behind(): return lax.ppermute(x, axis, pairs)  4.3 us
    reduce_sum x6, other arithmetic, window_stack(): centred = values - jnp.mean(values, axis=1, keepdims=True)  3.52 us
  transfers between devices with their start and end apart: 5, of which 2 were waited for; matrix products, arithmetic and copies ran while one was open for 24% of the time, Pallas kernels for 0%

commit v1 on v0

--- a/solution.py
+++ b/solution.py
@@ -90,7 +90,9 @@
     groups = lax.axis_size("tm")
     group_cols = ASSETS // (2 * groups)
     outgoing = tick_bars.reshape(groups, 1, -1)
-    arrived = lax.all_to_all(outgoing, "tm", split_axis=0, concat_axis=1, tiled=True)
+    parts = jnp.split(outgoing, lax.axis_size("tm"), axis=0)
+    incoming = lax.all_to_all(jnp.stack(parts), "tm", 0, 0)
+    arrived = jnp.concatenate(incoming, axis=1)
     block_len = arrived.shape[2] // group_cols
     own_rows = jnp.transpose(arrived.reshape(groups, block_len, group_cols), (1, 0, 2)).reshape(
         block_len, groups * group_cols

time: 133 us -> 155 us (1.17)
  local copies, waits for them, and re-layouts: 12.9 us -> 33.9 us
    unnamed x10 -> x25, local copies, waits for them, and re-layouts: 0.72 us -> 20.4 us
  transfers between devices with their start and end apart: 5 -> 5, of which waited for: 2 -> 2; matrix products, arithmetic and copies ran while one was open for 24% -> 21% of each run, Pallas kernels for 0% -> 0%
where the time goes in v1:
time: 155 us; the launch traced here: 154 us
  matrix products  45.7 us (29%)
  local copies, waits for them, and re-layouts  33.9 us (22%)
  waiting for transfers between devices  28 us (18%)
  blocking collectives  22.3 us (14%)
  starting transfers between devices  15 us (10%)
  other arithmetic  7.66 us (5%)
    dot_general x24, matrix products, block_magnitude(): lax.dot_general(left_part[:, offset:offset + block_rows], right_part, (((...  45.7 us
    all_gather x1, blocking collectives, time_block_rows(): prior_all = lax.all_gather(prior_bars, 'tm', axis=1, tiled=True)  22.3 us
    unnamed x25, local copies, waits for them, and re-layouts  20.4 us
    ppermute x2, waiting for transfers between devices, swapped(): return lax.ppermute(block, axis, route)  18.2 us
    all_to_all x1, waiting for transfers between devices, time_block_rows(): incoming = lax.all_to_all(jnp.stack(parts), 'tm', 0, 0)  9.75 us
    all_to_all x1, starting transfers between devices, time_block_rows(): incoming = lax.all_to_all(jnp.stack(parts), 'tm', 0, 0)  7.55 us
    another operation x7, local copies, waits for them, and re-layouts, window_stack(): jnp.stack([groups[offset:offset + WIN_DEV] for offset in range(SPAN // ST...  7.1 us
    ppermute x2, starting transfers between devices, from_behind(): return lax.ppermute(x, axis, pairs)  4.3 us
  transfers between devices with their start and end apart: 5, of which 2 were waited for; matrix products, arithmetic and copies ran while one was open for 21% of the time, Pallas kernels for 0%

profile of v1, /device:TPU:0, one launch (start us, length us, event | category | flops | bytes accessed | tf_op | source)
XLA Modules:
  0.0 153.5 jit_solution(6855125434389436277)
XLA Ops:
  0.0 1.3 constant_dynamic-update-slice_fusion.15
  1.3 1.3 constant_dynamic-update-slice_fusion.14
  2.6 1.3 constant_dynamic-update-slice_fusion.13
  3.9 1.3 constant_dynamic-update-slice_fusion.12
  5.3 1.3 constant_dynamic-update-slice_fusion.11
  6.6 1.3 constant_dynamic-update-slice_fusion.10
  7.9 1.3 constant_dynamic-update-slice_fusion.9
  9.2 1.3 constant_dynamic-update-slice_fusion.8
  10.5 1.3 constant_dynamic-update-slice_fusion.7
  11.8 1.3 constant_dynamic-update-slice_fusion.6
  13.2 1.3 constant_dynamic-update-slice_fusion.5
  14.5 1.3 constant_dynamic-update-slice_fusion.4
  15.8 1.3 constant_dynamic-update-slice_fusion.3
  17.1 1.3 constant_dynamic-update-slice_fusion.2
  18.4 1.3 constant_dynamic-update-slice_fusion.1
  19.7 1.3 constant_dynamic-update-slice_fusion
  21.0 7.5 %all-to-all-start = ((f32[16,1,1,3840]{3,2,1,0:T(1,128)}), f32[16,1,1,3840]{3,2,1,0:T(1,128)S(1)}, u32[]{:S(2)}, u32[]{:S(2)}) async-start(f32[16,1,1,3840]{3,2,1,0:T(1,128)} %constant_dynamic-update-slice_fusion), calls=%async_computation | async-start | bytes 491520 | tf_op jit(solution)/shard_map/all_to_all | solution.py:94
  28.6 9.8 %all-to-all-done = f32[16,1,1,3840]{3,2,1,0:T(1,128)S(1)} async-done(((f32[16,1,1,3840]{3,2,1,0:T(1,128)}), f32[16,1,1,3840]{3,2,1,0:T(1,128)S(1)}, u32[]{:S(2)}, u32[]{:S(2)}) %all-to-all-start) | async-done | bytes 245792 | tf_op jit(solution)/shard_map/all_to_all | solution.py:94
  38.4 0.6 reduce.9
  39.4 1.8 %collective-permute-start.1 = (f32[15,4096]{1,0:T(8,128)S(1)}, f32[15,4096]{1,0:T(8,128)S(1)}, u32[]{:S(2)}, u32[]{:S(2)}) collective-permute-start(f32[15,4096]{1,0:T(8,128)S(1)} %bitcast.117), channel_id=1, source_target_pairs={{0,2},{2,4},{4,6},{6,8},{8,10},{10,12},{12,14},{14,16},{16,18},{18... | collective-permute-start | bytes 737288 | tf_op jit(solution)/shard_map/ppermute | solution.py:18
  41.5 2.5 %collective-permute-start = (f32[10,4096]{1,0:T(8,128)S(1)}, f32[10,4096]{1,0:T(8,128)S(1)}, u32[]{:S(2)}, u32[]{:S(2)}) collective-permute-start(f32[10,4096]{1,0:T(8,128)S(1)} %bitcast.123), channel_id=1, source_target_pairs={{0,4},{2,6},{4,8},{6,10},{8,12},{10,14},{12,16},{14,18},{16,20},{1... | collective-permute-start | bytes 491528 | tf_op jit(solution)/shard_map/ppermute | solution.py:18
  44.0 22.3 %all_gather.3 = f32[1,16,6400]{2,0,1:T(1,128)S(1)} all-gather(f32[1,1,6400]{2,0,1:T(1,128)S(1)} %bitcast.124), channel_id=1, replica_groups=mesh['tm'=16,'asset'=2] {'tm'}, dimensions={1}, use_global_device_ids=true | all-gather | bytes 435200 | tf_op jit(solution)/shard_map/all_gather | solution.py:100
  66.4 1.0 reduce.8
  68.3 1.1 pad_maximum_fusion.3
  69.4 0.8 fusion.25
  70.2 1.7 %stack.90 = f32[3,1,5,4096]{3,2,0,1:T(8,128)} reshape(f32[15,4096]{1,0:T(8,128)} %get-tuple-element.124) | data formatting | bytes 491520 | tf_op jit(solution)/shard_map/stack | solution.py:34
  71.9 1.7 %stack.91 = f32[3,1,5,4096]{3,2,0,1:T(8,128)} reshape(f32[15,4096]{1,0:T(8,128)} %get-tuple-element.123) | data formatting | bytes 491520 | tf_op jit(solution)/shard_map/stack | solution.py:34
  73.6 1.0 stack.92
  74.6 1.0 stack.93
  75.6 1.1 fusion.24
  76.7 1.1 fusion.26
  78.4 1.6 %copy.13 = f32[3,6,5,4096]{3,2,1,0:T(8,128)} copy(f32[3,6,5,4096]{3,2,0,1:T(8,128)S(1)} %get-tuple-element.137) | data formatting | bytes 2949120 | tf_op jit(solution)/shard_map/stack | solution.py:34
  80.4 1.7 %reshape.107 = f32[3,30,4096]{2,1,0:T(8,128)S(1)} reshape(f32[3,6,5,4096]{3,2,1,0:T(8,128)} %copy.13) | data formatting | bytes 2949120 | tf_op jit(solution)/shard_map/reshape | solution.py:37
  82.3 1.6 %collective-permute-start.2 = (bf16[3,30,4096]{2,1,0:T(8,128)(2,1)S(1)}, bf16[3,30,4096]{2,1,0:T(8,128)(2,1)S(1)}, u32[]{:S(2)}, u32[]{:S(2)}) collective-permute-start(bf16[3,30,4096]{2,1,0:T(8,128)(2,1)S(1)} %multiply_convert_fusion), channel_id=1, source_target_pairs={{0,1},{1,0},{2,3},{3,2},{4,5},{5,4},{6,7},{7,6},{8,9},{9,8},{10,11... | collective-permute-start | bytes 2211848 | tf_op jit(solution)/shard_map/ppermute | solution.py:28
  84.0 18.2 %collective-permute-done.2 = bf16[3,30,4096]{2,1,0:T(8,128)(2,1)S(1)} collective-permute-done((bf16[3,30,4096]{2,1,0:T(8,128)(2,1)S(1)}, bf16[3,30,4096]{2,1,0:T(8,128)(2,1)S(1)}, u32[]{:S(2)}, u32[]{:S(2)}) %collective-permute-start.2) | collective-permute-done | bytes 737312 | tf_op jit(solution)/shard_map/ppermute | solution.py:28
  102.3 9.1 %while.35 = (s32[]{:T(128)}, f32[3,2048]{1,0:T(4,128)S(1)}, f32[3,2048]{1,0:T(4,128)S(1)}, bf16[3,30,2048]{2,1,0:T(8,128)(2,1)S(1)}, bf16[3,30,2048]{2,1,0:T(8,128)(2,1)S(1)}, /*index=5*/s32[]{:T(128)}, s32[]{:T(128)}) while((s32[]{:T(128)}, f32[3,2048]{1,0:T(4,128)S(1)}, f32[3,2048]{1,0:T(4,128)S(1)}, bf16[3,30,2048]{2,1,0:T(8,128)(2,1)S(1)}, ...), condition=%wide.region_18.19_spmd, body=%wide.region_13.18_spmd.sunk | while | flops 272627712 | bytes 737377 | solution.py:82
  102.3 1.4 convert_reduce_fusion.25
  103.7 1.4 convert_reduce_fusion.24
  105.4 1.4 convert_reduce_fusion.25
  106.7 1.4 convert_reduce_fusion.24
  108.4 1.4 convert_reduce_fusion.25
  109.8 1.4 convert_reduce_fusion.24
  111.5 9.2 %while.36 = (s32[]{:T(128)}, f32[3,2048]{1,0:T(4,128)S(1)}, f32[3,2048]{1,0:T(4,128)S(1)}, bf16[3,30,2048]{2,1,0:T(8,128)(2,1)S(1)}, bf16[3,30,2048]{2,1,0:T(8,128)(2,1)S(1)}, /*index=5*/s32[]{:T(128)}, s32[]{:T(128)}) while((s32[]{:T(128)}, f32[3,2048]{1,0:T(4,128)S(1)}, f32[3,2048]{1,0:T(4,128)S(1)}, bf16[3,30,2048]{2,1,0:T(8,128)(2,1)S(1)}, ...), condition=%wide.region_24.25_spmd, body=%wide.region_19.24_spmd.sunk | while | flops 272627712 | bytes 737377 | solution.py:82
  111.5 1.4 convert_reduce_fusion.27
  112.9 1.4 convert_reduce_fusion.26
  114.6 1.4 convert_reduce_fusion.27
  115.9 1.4 convert_reduce_fusion.26
  117.6 1.4 convert_reduce_fusion.27
  119.0 1.4 convert_reduce_fusion.26
  120.7 1.6 %collective-permute-start.3 = (bf16[3,4096]{1,0:T(4,128)(2,1)S(1)}, bf16[3,4096]{1,0:T(4,128)(2,1)S(1)}, u32[]{:S(2)}, u32[]{:S(2)}) collective-permute-start(bf16[3,4096]{1,0:T(4,128)(2,1)S(1)} %convert_element_type.58), channel_id=1, source_target_pairs={{0,1},{1,0},{2,3},{3,2},{4,5},{5,4},{6,7},{7,6},{8,9},{9,8},{10,11... | collective-permute-start | bytes 73736 | tf_op jit(solution)/shard_map/ppermute | solution.py:28
  122.3 30.5 %while.34 = (s32[]{:T(128)}, f32[3,4096]{1,0:T(4,128)S(1)}, bf16[3,30,4096]{2,1,0:T(8,128)(2,1)S(1)}, s32[]{:T(128)}, s32[]{:T(128)}) while((s32[]{:T(128)}, f32[3,4096]{1,0:T(4,128)S(1)}, bf16[3,30,4096]{2,1,0:T(8,128)(2,1)S(1)}, s32[]{:T(128)}, s32[]{:T(128)}) %tuple.68), condition=%wide.region_12.13_spmd, body=%wide.region_7.12_spmd.sunk | while | flops 1073750016 | bytes 1884229 | solution.py:65
  122.6 2.4 %convert_reduce_fusion.20 = f32[1024]{0:T(1024)S(1)} fusion(bf16[30,4096]{1,0:T(8,128)(2,1)S(1)} %dynamic-slice_bitcast_fusion.6), kind=kOutput, calls=%fused_computation.clone.1 | convolution fusion | flops 268434432 | bytes 331776 | tf_op jit(solution)/shard_map/while/body/eval_jaxpr/dot_general | solution.py:44
  125.0 2.5 %convert_reduce_fusion.21 = f32[1024]{0:T(1024)S(1)} fusion(bf16[30,4096]{1,0:T(8,128)(2,1)S(1)} %dynamic-slice_bitcast_fusion.6), kind=kOutput, calls=%fused_computation.1.clone.1 | convolution fusion | flops 268434432 | bytes 331776 | tf_op jit(solution)/shard_map/while/body/eval_jaxpr/dot_general | solution.py:44
  127.5 2.5 %convert_reduce_fusion.22 = f32[1024]{0:T(1024)S(1)} fusion(bf16[30,4096]{1,0:T(8,128)(2,1)S(1)} %dynamic-slice_bitcast_fusion.6), kind=kOutput, calls=%fused_computation.2.clone.1 | convolution fusion | flops 268434432 | bytes 331776 | tf_op jit(solution)/shard_map/while/body/eval_jaxpr/dot_general | solution.py:44
  129.9 2.5 %convert_reduce_fusion.23 = f32[1024]{0:T(1024)S(1)} fusion(bf16[30,4096]{1,0:T(8,128)(2,1)S(1)} %dynamic-slice_bitcast_fusion.6), kind=kOutput, calls=%fused_computation.3.clone.1 | convolution fusion | flops 268434432 | bytes 331776 | tf_op jit(solution)/shard_map/while/body/eval_jaxpr/dot_general | solution.py:44
  132.7 2.4 %convert_reduce_fusion.20 = f32[1024]{0:T(1024)S(1)} fusion(bf16[30,4096]{1,0:T(8,128)(2,1)S(1)} %dynamic-slice_bitcast_fusion.6), kind=kOutput, calls=%fused_computation.clone.1 | convolution fusion | flops 268434432 | bytes 331776 | tf_op jit(solution)/shard_map/while/body/eval_jaxpr/dot_general | solution.py:44
  135.1 2.5 %convert_reduce_fusion.21 = f32[1024]{0:T(1024)S(1)} fusion(bf16[30,4096]{1,0:T(8,128)(2,1)S(1)} %dynamic-slice_bitcast_fusion.6), kind=kOutput, calls=%fused_computation.1.clone.1 | convolution fusion | flops 268434432 | bytes 331776 | tf_op jit(solution)/shard_map/while/body/eval_jaxpr/dot_general | solution.py:44
  137.6 2.5 %convert_reduce_fusion.22 = f32[1024]{0:T(1024)S(1)} fusion(bf16[30,4096]{1,0:T(8,128)(2,1)S(1)} %dynamic-slice_bitcast_fusion.6), kind=kOutput, calls=%fused_computation.2.clone.1 | convolution fusion | flops 268434432 | bytes 331776 | tf_op jit(solution)/shard_map/while/body/eval_jaxpr/dot_general | solution.py:44
  140.0 2.5 %convert_reduce_fusion.23 = f32[1024]{0:T(1024)S(1)} fusion(bf16[30,4096]{1,0:T(8,128)(2,1)S(1)} %dynamic-slice_bitcast_fusion.6), kind=kOutput, calls=%fused_computation.3.clone.1 | convolution fusion | flops 268434432 | bytes 331776 | tf_op jit(solution)/shard_map/while/body/eval_jaxpr/dot_general | solution.py:44
  142.8 2.4 %convert_reduce_fusion.20 = f32[1024]{0:T(1024)S(1)} fusion(bf16[30,4096]{1,0:T(8,128)(2,1)S(1)} %dynamic-slice_bitcast_fusion.6), kind=kOutput, calls=%fused_computation.clone.1 | convolution fusion | flops 268434432 | bytes 331776 | tf_op jit(solution)/shard_map/while/body/eval_jaxpr/dot_general | solution.py:44
  145.2 2.5 %convert_reduce_fusion.21 = f32[1024]{0:T(1024)S(1)} fusion(bf16[30,4096]{1,0:T(8,128)(2,1)S(1)} %dynamic-slice_bitcast_fusion.6), kind=kOutput, calls=%fused_computation.1.clone.1 | convolution fusion | flops 268434432 | bytes 331776 | tf_op jit(solution)/shard_map/while/body/eval_jaxpr/dot_general | solution.py:44
  147.7 2.5 %convert_reduce_fusion.22 = f32[1024]{0:T(1024)S(1)} fusion(bf16[30,4096]{1,0:T(8,128)(2,1)S(1)} %dynamic-slice_bitcast_fusion.6), kind=kOutput, calls=%fused_computation.2.clone.1 | convolution fusion | flops 268434432 | bytes 331776 | tf_op jit(solution)/shard_map/while/body/eval_jaxpr/dot_general | solution.py:44
  150.1 2.5 %convert_reduce_fusion.23 = f32[1024]{0:T(1024)S(1)} fusion(bf16[30,4096]{1,0:T(8,128)(2,1)S(1)} %dynamic-slice_bitcast_fusion.6), kind=kOutput, calls=%fused_computation.3.clone.1 | convolution fusion | flops 268434432 | bytes 331776 | tf_op jit(solution)/shard_map/while/body/eval_jaxpr/dot_general | solution.py:44
  152.9 0.7 fusion.22
  (80 shorter events, 5.5 us)
Async XLA Ops:
  21.0 23.0 %copy-start.1 = (f32[1,1,6400]{2,1,0:T(1,128)S(1)}, f32[1,1,6400]{2,1,0:T(1,128)}, u32[]{:S(2)}) copy-start(f32[1,1,6400]{2,1,0:T(1,128)} %param.9) | copy-start | bytes 76804
  21.0 17.3 %all-to-all-start = ((f32[16,1,1,3840]{3,2,1,0:T(1,128)}), f32[16,1,1,3840]{3,2,1,0:T(1,128)S(1)}, u32[]{:S(2)}, u32[]{:S(2)}) async-start(f32[16,1,1,3840]{3,2,1,0:T(1,128)} %constant_dynamic-update-slice_fusion), calls=%async_computation | async-start | bytes 491520 | tf_op jit(solution)/shard_map/all_to_all | solution.py:94
  39.4 28.7 %collective-permute-start.1 = (f32[15,4096]{1,0:T(8,128)S(1)}, f32[15,4096]{1,0:T(8,128)S(1)}, u32[]{:S(2)}, u32[]{:S(2)}) collective-permute-start(f32[15,4096]{1,0:T(8,128)S(1)} %bitcast.117), channel_id=1, source_target_pairs={{0,2},{2,4},{4,6},{6,8},{8,10},{10,12},{12,14},{14,16},{16,18},{18... | collective-permute-start | bytes 737288 | tf_op jit(solution)/shard_map/ppermute | solution.py:18
  41.5 26.6 %collective-permute-start = (f32[10,4096]{1,0:T(8,128)S(1)}, f32[10,4096]{1,0:T(8,128)S(1)}, u32[]{:S(2)}, u32[]{:S(2)}) collective-permute-start(f32[10,4096]{1,0:T(8,128)S(1)} %bitcast.123), channel_id=1, source_target_pairs={{0,4},{2,6},{4,8},{6,10},{8,12},{10,14},{12,16},{14,18},{16,20},{1... | collective-permute-start | bytes 491528 | tf_op jit(solution)/shard_map/ppermute | solution.py:18
  78.3 1.6 %copy-start = (f32[3,4096]{1,0:T(4,128)S(1)}, f32[3,4096]{1,0:T(4,128)}, u32[]{:S(2)}) copy-start(f32[3,4096]{1,0:T(4,128)} %get-tuple-element.128) | copy-start | bytes 147460
  82.3 19.9 %collective-permute-start.2 = (bf16[3,30,4096]{2,1,0:T(8,128)(2,1)S(1)}, bf16[3,30,4096]{2,1,0:T(8,128)(2,1)S(1)}, u32[]{:S(2)}, u32[]{:S(2)}) collective-permute-start(bf16[3,30,4096]{2,1,0:T(8,128)(2,1)S(1)} %multiply_convert_fusion), channel_id=1, source_target_pairs={{0,1},{1,0},{2,3},{3,2},{4,5},{5,4},{6,7},{7,6},{8,9},{9,8},{10,11... | collective-permute-start | bytes 2211848 | tf_op jit(solution)/shard_map/ppermute | solution.py:28
  120.7 32.1 %collective-permute-start.3 = (bf16[3,4096]{1,0:T(4,128)(2,1)S(1)}, bf16[3,4096]{1,0:T(4,128)(2,1)S(1)}, u32[]{:S(2)}, u32[]{:S(2)}) collective-permute-start(bf16[3,4096]{1,0:T(4,128)(2,1)S(1)} %convert_element_type.58), channel_id=1, source_target_pairs={{0,1},{1,0},{2,3},{3,2},{4,5},{5,4},{6,7},{7,6},{8,9},{9,8},{10,11... | collective-permute-start | bytes 73736 | tf_op jit(solution)/shard_map/ppermute | solution.py:28
